TPU v7x, 32 devices: a 4x2x2 block of a 4x4x8 slice. The times are simulated.
32 devices in a mesh: sys: 4 (over y, z), seg: 8 (over x, core).
Axes of the slice: x: 4, y: 2, z: 2, core: 2. Of those that a mesh axis runs over, the one named last changes fastest.
The devices are a block of a 4x4x8 slice.
Arguments:
- positions: bfloat16 [98304, 512], P(('sys', 'seg')), parts along dimension 0
- charges: float32 [98304], P(('sys', 'seg')), parts along dimension 0
- pair_band: int32 [32, 7], P(('sys', 'seg')), parts along dimension 0
Outputs:
- output 1: float32 [98304, 512], P(('sys', 'seg')), parts along dimension 0
- output 2: float32 [4], P('sys'), parts along dimension 0
There are 4 independent parts. A program takes and returns all parts, laid end to end along the dimension named above; each array names one.
All inputs are finite; a program needn't handle non-finite values.
Results may differ from a plain program's by a relative error of at most 0.001.
Values are sent between devices in bfloat16 or wider.
A program may use at most 768 MiB of HBM per device.

v0:
```python
import jax
import jax.numpy as jnp
from jax import lax
from jax.sharding import PartitionSpec as P


def solution(mesh):
    seg_len = mesh.shape['seg']
    fwd_perm = [(src_dev, (src_dev + 1) % seg_len) for src_dev in range(seg_len)]

    def device_fn(positions, charges, pair_band):
        n_rows, feat_dim = positions.shape
        reach_steps = (pair_band.shape[1] - 1) // 2
        inv_lsq = 1.0 / feat_dim
        band_row = pair_band[0]
        row_ids = jnp.arange(n_rows)
        host_sq = jnp.einsum('nd,nd->n', positions, positions, preferred_element_type=jnp.float32)

        def pair_weights(x_vis, q_vis, sq_vis):
            cross_dot = jnp.einsum('id,jd->ij', positions, x_vis, preferred_element_type=jnp.float32)
            sq_dist = jnp.maximum(host_sq[:, None] + sq_vis[None, :] - 2.0 * cross_dot, 0.0)
            return charges[:, None] * q_vis[None, :] * jnp.exp(sq_dist * (-0.5 * inv_lsq))

        self_w = jnp.where(row_ids[:, None] == row_ids[None, :], 0.0, pair_weights(positions, charges, host_sq))
        self_pull = jnp.dot(self_w.astype(jnp.bfloat16), positions, preferred_element_type=jnp.float32)
        forces = (jnp.sum(self_w, axis=1)[:, None] * positions - self_pull) * inv_lsq
        energy = 0.5 * jnp.sum(self_w)

        def live_pair(operands):
            x_vis, q_vis = operands
            sq_vis = jnp.einsum('nd,nd->n', x_vis, x_vis, preferred_element_type=jnp.float32)
            weights = pair_weights(x_vis, q_vis, sq_vis)
            w_low = weights.astype(jnp.bfloat16)
            host_pull = jnp.dot(w_low, x_vis, preferred_element_type=jnp.float32)
            vis_pull = jnp.einsum('ij,id->jd', w_low, positions, preferred_element_type=jnp.float32)
            host_part = (jnp.sum(weights, axis=1)[:, None] * positions - host_pull) * inv_lsq
            vis_part = (jnp.sum(weights, axis=0)[:, None] * x_vis - vis_pull) * inv_lsq
            return host_part, vis_part, jnp.sum(weights)

        def dead_pair(operands):
            zero_rows = jnp.zeros((n_rows, feat_dim), jnp.float32)
            return zero_rows, zero_rows, jnp.zeros((), jnp.float32)

        x_vis, q_vis = positions, charges
        react_acc = jnp.zeros((n_rows, feat_dim), jnp.float32)
        for step_idx in range(1, reach_steps + 1):
            x_vis = lax.ppermute(x_vis, 'seg', fwd_perm)
            q_vis = lax.ppermute(q_vis, 'seg', fwd_perm)
            if step_idx > 1:
                react_acc = lax.ppermute(react_acc, 'seg', fwd_perm)
            host_part, vis_part, pair_energy = lax.cond(band_row[reach_steps - step_idx] != 0, live_pair, dead_pair, (x_vis, q_vis))
            forces = forces + host_part
            react_acc = react_acc + vis_part
            energy = energy + pair_energy
        back_perm = [(src_dev, (src_dev - reach_steps) % seg_len) for src_dev in range(seg_len)]
        forces = forces + lax.ppermute(react_acc, 'seg', back_perm)
        energy = lax.psum(energy, 'seg')
        return forces, energy.reshape(1)

    row_spec = P(('sys', 'seg'), None)
    vec_spec = P(('sys', 'seg'))
    return jax.shard_map(device_fn, mesh=mesh, in_specs=(row_spec, vec_spec, row_spec), out_specs=(row_spec, P('sys')), check_vma=False)
```

profile of v0, /device:TPU:81, one launch (start us, length us, event | category | flops | bytes accessed | tf_op | source)
XLA Modules:
  0.0 604.2 jit_solution(3741229897398871684)
XLA Ops:
  0.6 2.7 collective-permute-start.1
  3.3 0.1 collective-permute-start
  3.4 2.6 fusion.35
  6.0 1.4 fusion.46
  8.0 29.6 %collective-permute-done = f32[3072]{0:T(1024)S(1)} collective-permute-done((f32[3072]{0:T(1024)}, f32[3072]{0:T(1024)S(1)}, u32[]{:S(2)}, u32[]{:S(2)}) %collective-permute-start) | collective-permute-done | bytes 12320 | tf_op jit(solution)/shard_map/ppermute | solution.py:48
  37.7 0.0 collective-permute-done.1
  37.7 0.0 copy-start.5
  37.7 1.6 copy-done.5
  39.3 15.5 %conditional.3 = (f32[3072,512]{1,0:T(8,128)}, f32[3072,512]{1,0:T(8,128)}, f32[]{:T(128)}) conditional(s32[]{:T(128)} %bitcast, () %tuple.32, (f32[3072]{0:T(1024)}, f32[3072]{0:T(1024)S(1)}, f32[3072]{0:T(1024)S(1)}, bf16[3072,512]{1,0:T(8,128)(2,1)S(1)}, bf16[3072,512]{1,0:T(8,128)(2,1)}) %tuple.33), branch_computations={%region_1.2_spmd, %region_2.6_spmd} | conditional | flops 29112131584 | bytes 103919672 | solution.py:51
  39.3 3.5 broadcast.60
  42.8 3.5 broadcast.60.clone
  54.8 46.7 %collective-permute-start.6 = (f32[3072,512]{1,0:T(8,128)}, f32[3072,512]{1,0:T(8,128)}, u32[]{:S(2)}, u32[]{:S(2)}) collective-permute-start(f32[3072,512]{1,0:T(8,128)} %get-tuple-element.59), channel_id=1, source_target_pairs={{0,1},{1,2},{2,3},{3,4},{4,5},{5,6},{6,7},{7,0},{8,9},{9,10},{10,1... | collective-permute-start | bytes 18874376 | tf_op jit(solution)/shard_map/ppermute | solution.py:50
  101.5 0.1 collective-permute-start.3
  101.5 0.1 collective-permute-start.2
  102.3 101.0 %collective-permute-done.2 = f32[3072]{0:T(1024)S(1)} collective-permute-done((f32[3072]{0:T(1024)S(1)}, f32[3072]{0:T(1024)S(1)}, u32[]{:S(2)}, u32[]{:S(2)}) %collective-permute-start.2) | collective-permute-done | bytes 12320 | tf_op jit(solution)/shard_map/ppermute | solution.py:48
  203.2 0.0 collective-permute-done.3
  203.2 0.0 copy-start.3
  203.2 1.7 copy-done.3
  204.9 9.7 %conditional.4 = (f32[3072,512]{1,0:T(8,128)}, f32[3072,512]{1,0:T(8,128)}, f32[]{:T(128)}) conditional(s32[]{:T(128)} %bitcast.1, () %tuple.34, (f32[3072]{0:T(1024)}, f32[3072]{0:T(1024)S(1)}, f32[3072]{0:T(1024)S(1)}, bf16[3072,512]{1,0:T(8,128)(2,1)S(1)}, bf16[3072,512]{1,0:T(8,128)(2,1)}) %tuple.35), branch_computations={%region_6.0_spmd, %region_7.11_spmd} | conditional | flops 29112131584 | bytes 103919672 | solution.py:51
  204.9 3.5 broadcast.65
  208.4 3.5 broadcast.65.clone
  214.7 0.0 collective-permute-done.6
  214.7 0.0 copy-start.4
  214.7 0.0 copy-start
  214.7 0.0 copy-start.6
  214.7 9.1 %add.87 = f32[3072,512]{1,0:T(8,128)} add(f32[3072,512]{1,0:T(8,128)} %collective-permute-done.6, f32[3072,512]{1,0:T(8,128)} %get-tuple-element.60) | non-fusion elementwise | flops 1572864 | bytes 18874368 | tf_op jit(solution)/shard_map/add | solution.py:53
  223.8 52.2 %collective-permute-start.7 = (f32[3072,512]{1,0:T(8,128)}, f32[3072,512]{1,0:T(8,128)}, u32[]{:S(2)}, u32[]{:S(2)}) collective-permute-start(f32[3072,512]{1,0:T(8,128)} %add.87), channel_id=1, source_target_pairs={{0,1},{1,2},{2,3},{3,4},{4,5},{5,6},{6,7},{7,0},{8,9},{9,10},{10,1... | collective-permute-start | bytes 18874376 | tf_op jit(solution)/shard_map/ppermute | solution.py:50
  276.0 0.0 copy-done.4
  276.0 0.0 collective-permute-start.5
  276.1 0.1 collective-permute-start.4
  276.8 101.0 %collective-permute-done.4 = f32[3072]{0:T(1024)S(1)} collective-permute-done((f32[3072]{0:T(1024)S(1)}, f32[3072]{0:T(1024)S(1)}, u32[]{:S(2)}, u32[]{:S(2)}) %collective-permute-start.4) | collective-permute-done | bytes 12320 | tf_op jit(solution)/shard_map/ppermute | solution.py:48
  377.8 0.0 collective-permute-done.5
  377.8 0.0 copy-done
  377.8 0.0 copy-done.6
  377.8 57.4 %conditional.5 = (f32[3072,512]{1,0:T(8,128)}, f32[3072,512]{1,0:T(8,128)}, f32[]{:T(128)}) conditional(s32[]{:T(128)} %bitcast.2, () %tuple.36, (f32[3072]{0:T(1024)S(1)}, f32[3072]{0:T(1024)S(1)}, f32[3072]{0:T(1024)S(1)}, bf16[3072,512]{1,0:T(8,128)(2,1)S(1)}, bf16[3072,512]{1,0:T(8,128)(2,1)S(1)}) %tuple.63), branch_computations={%region_11.0_spmd, %region_12.16_spmd} | conditional | flops 29112131584 | bytes 91336728 | solution.py:51
  378.3 0.7 fusion.26
  379.0 23.4 %fusion.44 = (f32[]{:T(128)}, f32[3072]{0:T(1024)S(1)}, f32[3072]{0:T(1024)S(1)}, bf16[3072,3072]{1,0:T(8,128)(2,1)}) fusion(bf16[3072,512]{1,0:T(8,128)(2,1)S(1)} %get-tuple-element.44, bf16[3072,512]{1,0:T(8,128)(2,1)S(1)} %get-tuple-element.43, f32[3072]{0:T(1024)S(1)} %fusion.26, f32[3072]{0:T(1024)S(1)} %get-tuple-element.42, ...), kind=kOutput, calls=%fused_computation.48 | convolution fusion | flops 9767479296 | bytes 25239556 | tf_op jit(solution)/shard_map/cond/branch_1_fun/id,jd->ij/dot_general | solution.py:20
  402.4 16.1 %fusion.28 = f32[3072,512]{1,0:T(8,128)} fusion(bf16[3072,512]{1,0:T(8,128)(2,1)S(1)} %get-tuple-element.43, bf16[3072,512]{1,0:T(8,128)(2,1)S(1)} %get-tuple-element.44, bf16[3072,3072]{1,0:T(8,128)(2,1)} %get-tuple-element.78, f32[3072]{0:T(1024)S(1)} %get-tuple-element.72), kind=kOutput, calls=%fused_computation.31 | convolution fusion | flops 9669967872 | bytes 31469568 | tf_op jit(solution)/shard_map/cond/branch_1_fun/ij,id->jd/dot_general | solution.py:35
  418.5 15.9 %subtract_multiply_fusion.2 = f32[3072,512]{1,0:T(8,128)} fusion(bf16[3072,512]{1,0:T(8,128)(2,1)S(1)} %get-tuple-element.44, bf16[3072,512]{1,0:T(8,128)(2,1)S(1)} %get-tuple-element.43, bf16[3072,3072]{1,0:T(8,128)(2,1)} %get-tuple-element.78, f32[3072]{0:T(1024)S(1)} %get-tuple-element.73), kind=kOutput, calls=%fused_computation.32 | convolution fusion | flops 9669967872 | bytes 31469568 | tf_op jit(solution)/shard_map/cond/branch_1_fun/dot_general | solution.py:34
  435.2 0.0 collective-permute-done.7
  435.2 8.9 %add.88 = f32[3072,512]{1,0:T(8,128)} add(f32[3072,512]{1,0:T(8,128)} %collective-permute-done.7, f32[3072,512]{1,0:T(8,128)} %get-tuple-element.61) | non-fusion elementwise | flops 1572864 | bytes 18874368 | tf_op jit(solution)/shard_map/add | solution.py:53
  444.1 1.6 collective-permute-start.8
  445.7 26.9 %fusion.45 = (f32[]{:T(128)}, f32[3072]{0:T(1024)S(1)}, bf16[3072,3072]{0,1:T(8,128)(2,1)}) fusion(bf16[3072,512]{1,0:T(8,128)(2,1)S(1)} %copy-done, f32[3072]{0:T(1024)S(1)} %fusion.35, f32[3072]{0:T(1024)S(1)} %copy-done.6), kind=kOutput, calls=%fused_computation.49 | convolution fusion | flops 9776919552 | bytes 22056964 | tf_op jit(solution)/shard_map/id,jd->ij/dot_general | solution.py:20
  473.2 15.6 %fusion.33 = f32[3072,512]{1,0:T(8,128)} fusion(bf16[3072,512]{1,0:T(8,128)(2,1)S(1)} %copy-done, bf16[3072,3072]{0,1:T(8,128)(2,1)} %get-tuple-element.82), kind=kOutput, calls=%fused_computation.35 | convolution fusion | flops 9663676416 | bytes 28311552 | tf_op jit(solution)/shard_map/dot_general | solution.py:25
  488.8 101.4 %psum.7 = f32[1]{0:T(128)} all-reduce(f32[1]{0:T(128)} %bitcast.3), channel_id=1, replica_groups=mesh['sys'=4,'seg'=8] {'seg'}, use_global_device_ids=true, to_apply=%region_17.18 | all-reduce | flops 1 | bytes 8 | tf_op jit(solution)/shard_map/psum | solution.py:57
  590.2 0.0 collective-permute-done.8
  590.2 13.9 %fusion.41 = f32[3072,512]{1,0:T(8,128)} fusion(f32[3072,512]{1,0:T(8,128)} %collective-permute-done.8, f32[3072,512]{1,0:T(8,128)} %get-tuple-element.58, f32[3072,512]{1,0:T(8,128)} %get-tuple-element.57, f32[3072,512]{1,0:T(8,128)} %get-tuple-element.56, f32[3072,512]{1,0:T(8,128)} %fusion.33, bf16[3072,512]{1,0:T(8,128)(2,1)S(1)} %copy-done, ...), kind=kLoop, calls=%fused_computation.45 | loop fusion | flops 12582912 | bytes 40906752 | tf_op jit(solution)/shard_map/add | solution.py:56
Async XLA Ops:
  0.6 37.0 %collective-permute-start.1 = (bf16[3072,512]{1,0:T(8,128)(2,1)}, bf16[3072,512]{1,0:T(8,128)(2,1)S(1)}, u32[]{:S(2)}, u32[]{:S(2)}) collective-permute-start(bf16[3072,512]{1,0:T(8,128)(2,1)} %param.9), channel_id=1, source_target_pairs={{0,1},{1,2},{2,3},{3,4},{4,5},{5,6},{6,7},{7,0},{8,9},{9,10},{10,1... | collective-permute-start | bytes 9437192 | tf_op jit(solution)/shard_map/ppermute | solution.py:47
  3.3 34.3 %collective-permute-start = (f32[3072]{0:T(1024)}, f32[3072]{0:T(1024)S(1)}, u32[]{:S(2)}, u32[]{:S(2)}) collective-permute-start(f32[3072]{0:T(1024)} %param.10), channel_id=1, source_target_pairs={{0,1},{1,2},{2,3},{3,4},{4,5},{5,6},{6,7},{7,0},{8,9},{9,10},{10,1... | collective-permute-start | bytes 36872 | tf_op jit(solution)/shard_map/ppermute | solution.py:48
  37.7 1.6 copy-start.5
  54.8 159.9 %collective-permute-start.6 = (f32[3072,512]{1,0:T(8,128)}, f32[3072,512]{1,0:T(8,128)}, u32[]{:S(2)}, u32[]{:S(2)}) collective-permute-start(f32[3072,512]{1,0:T(8,128)} %get-tuple-element.59), channel_id=1, source_target_pairs={{0,1},{1,2},{2,3},{3,4},{4,5},{5,6},{6,7},{7,0},{8,9},{9,10},{10,1... | collective-permute-start | bytes 18874376 | tf_op jit(solution)/shard_map/ppermute | solution.py:50
  101.5 101.7 %collective-permute-start.3 = (bf16[3072,512]{1,0:T(8,128)(2,1)}, bf16[3072,512]{1,0:T(8,128)(2,1)S(1)}, u32[]{:S(2)}, u32[]{:S(2)}) collective-permute-start(bf16[3072,512]{1,0:T(8,128)(2,1)} %copy-done.5), channel_id=1, source_target_pairs={{0,1},{1,2},{2,3},{3,4},{4,5},{5,6},{6,7},{7,0},{8,9},{9,10},{10,1... | collective-permute-start | bytes 9437192 | tf_op jit(solution)/shard_map/ppermute | solution.py:47
  101.5 101.7 %collective-permute-start.2 = (f32[3072]{0:T(1024)S(1)}, f32[3072]{0:T(1024)S(1)}, u32[]{:S(2)}, u32[]{:S(2)}) collective-permute-start(f32[3072]{0:T(1024)S(1)} %collective-permute-done), channel_id=1, source_target_pairs={{0,1},{1,2},{2,3},{3,4},{4,5},{5,6},{6,7},{7,0},{8,9},{9,10},{10,1... | collective-permute-start | bytes 36872 | tf_op jit(solution)/shard_map/ppermute | solution.py:48
  203.2 1.7 copy-start.3
  214.7 61.3 %copy-start.4 = (bf16[3072,512]{1,0:T(8,128)(2,1)S(1)}, bf16[3072,512]{1,0:T(8,128)(2,1)}, u32[]{:S(2)}) copy-start(bf16[3072,512]{1,0:T(8,128)(2,1)} %copy-done.3) | copy-start | bytes 9437188
  214.7 163.1 %copy-start = (bf16[3072,512]{1,0:T(8,128)(2,1)S(1)}, bf16[3072,512]{1,0:T(8,128)(2,1)}, u32[]{:S(2)}) copy-start(bf16[3072,512]{1,0:T(8,128)(2,1)} %param.9) | copy-start | bytes 9437188
  214.7 163.1 %copy-start.6 = (f32[3072]{0:T(1024)S(1)}, f32[3072]{0:T(1024)}, u32[]{:S(2)}) copy-start(f32[3072]{0:T(1024)} %param.10) | copy-start | bytes 36868
  223.8 211.4 %collective-permute-start.7 = (f32[3072,512]{1,0:T(8,128)}, f32[3072,512]{1,0:T(8,128)}, u32[]{:S(2)}, u32[]{:S(2)}) collective-permute-start(f32[3072,512]{1,0:T(8,128)} %add.87), channel_id=1, source_target_pairs={{0,1},{1,2},{2,3},{3,4},{4,5},{5,6},{6,7},{7,0},{8,9},{9,10},{10,1... | collective-permute-start | bytes 18874376 | tf_op jit(solution)/shard_map/ppermute | solution.py:50
  276.0 101.7 %collective-permute-start.5 = (bf16[3072,512]{1,0:T(8,128)(2,1)S(1)}, bf16[3072,512]{1,0:T(8,128)(2,1)S(1)}, u32[]{:S(2)}, u32[]{:S(2)}) collective-permute-start(bf16[3072,512]{1,0:T(8,128)(2,1)S(1)} %copy-done.4), channel_id=1, source_target_pairs={{0,1},{1,2},{2,3},{3,4},{4,5},{5,6},{6,7},{7,0},{8,9},{9,10},{10,1... | collective-permute-start | bytes 9437192 | tf_op jit(solution)/shard_map/ppermute | solution.py:47
  276.1 101.7 %collective-permute-start.4 = (f32[3072]{0:T(1024)S(1)}, f32[3072]{0:T(1024)S(1)}, u32[]{:S(2)}, u32[]{:S(2)}) collective-permute-start(f32[3072]{0:T(1024)S(1)} %collective-permute-done.2), channel_id=1, source_target_pairs={{0,1},{1,2},{2,3},{3,4},{4,5},{5,6},{6,7},{7,0},{8,9},{9,10},{10,1... | collective-permute-start | bytes 36872 | tf_op jit(solution)/shard_map/ppermute | solution.py:48
  444.1 146.1 %collective-permute-start.8 = (f32[3072,512]{1,0:T(8,128)}, f32[3072,512]{1,0:T(8,128)}, u32[]{:S(2)}, u32[]{:S(2)}) collective-permute-start(f32[3072,512]{1,0:T(8,128)} %add.88), channel_id=1, source_target_pairs={{0,5},{1,6},{2,7},{3,0},{4,1},{5,2},{6,3},{7,4},{8,13},{9,14},{10,... | collective-permute-start | bytes 18874376 | tf_op jit(solution)/shard_map/ppermute | solution.py:56
where the time goes:
time: 613 us; the launch traced here: 604 us
  waiting for transfers between devices  232 us (38%)
  starting transfers between devices  103 us (17%)
  blocking collectives  101 us (16%)
  matrix products  97.9 us (16%)
  other arithmetic  35.2 us (6%)
  local copies, waits for them, and re-layouts  18.7 us (3%)
  loops' own time  12.5 us (2%)
    ppermute x3, waiting for transfers between devices, device_fn(): q_vis = lax.ppermute(q_vis, 'seg', fwd_perm)  232 us
    psum x1, blocking collectives, device_fn(): energy = lax.psum(energy, 'seg')  101 us
    ppermute x2, starting transfers between devices, device_fn(): react_acc = lax.ppermute(react_acc, 'seg', fwd_perm)  98.9 us
    dot_general x2, matrix products, pair_weights(): jnp.einsum('id,jd->ij', positions, x_vis, preferred_element_type=jnp.floa...  50.3 us
    add x2, other arithmetic, device_fn(): react_acc = react_acc + vis_part  18 us
    dot_general x1, matrix products, live_pair(): jnp.einsum('ij,id->jd', w_low, positions, preferred_element_type=jnp.floa...  16.1 us
    dot_general x1, matrix products, live_pair(): host_pull = jnp.dot(w_low, x_vis, preferred_element_type=jnp.float32)  15.9 us
    dot_general x1, matrix products, device_fn(): jnp.dot(self_w.astype(jnp.bfloat16), positions, preferred_element_type=jn...  15.6 us
  transfers between devices with their start and end apart: 9, of which 3 were waited for; matrix products, arithmetic and copies ran while one was open for 18% of the time, Pallas kernels for 0%

commit v1 on v0

v1 whole, which is shorter than its diff:
```python
import functools
import math

import jax
import jax.numpy as jnp
from jax import lax
from jax.experimental import pallas as pl
from jax.experimental.pallas import tpu as pltpu
from jax.sharding import PartitionSpec as P

MESH = pl.DeviceIdType.MESH
LANES = 128
CHUNKS = 6
ROW_TILE = 1024


def kernel(seg_len, reach, band_ref, x_hbm, q_ref, f_hbm, e_ref, x_all, meta, a_col, q_col, acc, row_acc, e_buf,
           local_sem, send_sem, recv_sem, msend_sem, mrecv_sem, esend_sem, erecv_sem, out_sem):
    n, d = x_hbm.shape
    chunk = n // CHUNKS
    me = lax.axis_index('seg')
    core = lax.rem(me, 2)
    mate = me + 1 - 2 * core
    right = lax.rem(me + 2, seg_len)
    left = lax.rem(me + seg_len - 2, seg_len)
    right_x = right + 1 - 2 * core
    left_x = left + 1 - 2 * core
    far_x = lax.rem(me + 4, seg_len) + 1 - 2 * core
    scale = math.log2(math.e) * 0.5 / d
    inv_lsq = 1.0 / d

    load = pltpu.make_async_copy(x_hbm, x_all.at[0], local_sem)
    load.start()

    barrier = pltpu.get_barrier_semaphore()
    for hop in range(1, seg_len):
        pl.semaphore_signal(barrier, inc=1, device_id={'seg': lax.rem(me + hop, seg_len)}, device_id_type=MESH)
    pl.semaphore_wait(barrier, seg_len - 1)

    def send(kind, k, src, slot, dev):
        rows = pl.ds(pl.multiple_of(k * chunk, chunk), chunk)
        return pltpu.make_async_remote_copy(
            src_ref=src.at[rows], dst_ref=x_all.at[slot, rows], send_sem=send_sem.at[kind, k],
            recv_sem=recv_sem.at[slot, k], device_id={'seg': dev}, device_id_type=MESH)

    def to_right(k):
        return send(0, k, x_hbm, 1, right)

    def to_left(k):
        return send(1, k, x_hbm, 2, left)

    def to_mate(k):
        return send(2, k, x_hbm, 6, mate)

    def pass_left_block(k):
        return send(3, k, x_all.at[1], 3, mate)

    def pass_right_block(k):
        return send(4, k, x_all.at[2], 4, mate)

    def pass_far(k):
        onward = core * right_x + (1 - core) * left_x
        return send(5, k, x_all.at[2 - core], 5, onward)

    to_right(0).start()
    to_left(0).start()
    load.wait()

    def prologue(r, _):
        rows = pl.ds(pl.multiple_of(r * LANES, LANES), LANES)
        x = x_all[0, rows, :].astype(jnp.float32)
        neg = jnp.sum(x * x, axis=1, keepdims=True) * (-scale)
        neg = jnp.broadcast_to(neg, (LANES, LANES))
        a_col[rows, :] = neg
        q_row = q_ref[:, rows]
        meta[0, 1:2, rows] = neg.T[0:1, :]
        meta[0, 0:1, rows] = q_row
        q_col[rows, :] = jnp.broadcast_to(q_row, (LANES, LANES)).T
        row_acc[rows, :] = jnp.zeros((LANES, LANES), jnp.float32)
        acc[rows, :] = jnp.zeros((LANES, d), jnp.float32)
        return 0

    lax.fori_loop(0, n // LANES, prologue, 0)

    to_mate(0).start()
    peers = ((1, right), (2, left), (3, right_x), (4, left_x), (5, far_x), (6, mate))
    metas = [
        pltpu.make_async_remote_copy(
            src_ref=meta.at[0], dst_ref=meta.at[slot], send_sem=msend_sem.at[slot], recv_sem=mrecv_sem.at[slot],
            device_id={'seg': dev}, device_id_type=MESH)
        for slot, dev in peers]
    for copy in metas:
        copy.start()

    def start_rest(k, _):
        to_right(k).start()
        to_left(k).start()
        to_mate(k).start()
        return 0

    lax.fori_loop(1, CHUNKS, start_rest, 0)

    def block_part(slot, k, column, own):
        cols = pl.ds(pl.multiple_of(k * chunk, chunk), chunk)
        live = band_ref[0, column] != 0
        q_row = jnp.where(live, meta[slot, 0:1, cols], 0.0)
        b_row = meta[slot, 1:2, cols]

        def row_tile(i, _):
            rows = pl.ds(pl.multiple_of(i * ROW_TILE, ROW_TILE), ROW_TILE)
            x_vis = x_all[slot, cols, :]
            dots = lax.dot_general(x_all[0, rows, :], x_vis, (((1,), (1,)), ((), ())),
                                   preferred_element_type=jnp.float32)
            a_tile = jnp.concatenate([a_col[rows, :]] * (chunk // LANES), axis=1)
            q_tile = jnp.concatenate([q_col[rows, :]] * (chunk // LANES), axis=1)
            weights = jnp.exp2(jnp.minimum((dots * (2.0 * scale) + a_tile) + b_row, 0.0)) * q_row * q_tile
            if own:
                row_id = lax.broadcasted_iota(jnp.int32, weights.shape, 0) + i * ROW_TILE
                col_id = lax.broadcasted_iota(jnp.int32, weights.shape, 1) + k * chunk
                weights = jnp.where(row_id == col_id, 0.0, weights)
            part = weights[:, 0:LANES]
            for s in range(1, chunk // LANES):
                part = part + weights[:, s * LANES:(s + 1) * LANES]
            row_acc[rows, :] += part
            acc[rows, :] += jnp.dot(weights.astype(jnp.bfloat16), x_vis, preferred_element_type=jnp.float32)
            return 0

        lax.fori_loop(0, n // ROW_TILE, row_tile, 0)

    def serve(k):
        to_right(k).wait_recv()
        to_left(k).wait_recv()
        pass_left_block(k).start()
        pass_right_block(k).start()
        pass_far(k).start()

    def own_part(k, _):
        block_part(0, k, reach, True)
        return 0

    lax.fori_loop(0, CHUNKS, own_part, 0)
    serve(0)
    for copy in metas:
        copy.wait_recv()

    def mate_part(k, _):
        to_mate(k).wait_recv()
        block_part(6, k, reach + 1 - 2 * core, False)
        return 0

    lax.fori_loop(0, CHUNKS, mate_part, 0)

    def ring_round(k, _):
        @pl.when(k + 1 < CHUNKS)
        def _():
            serve(k + 1)

        pass_left_block(k).wait_recv()
        pass_right_block(k).wait_recv()

        def ring_part(slot, _):
            direct = jnp.where(slot == 1, reach - 2, reach + 2)
            crossed = jnp.where(slot == 3, reach - 1 - 2 * core, reach + 3 - 2 * core)
            block_part(slot, k, jnp.where(slot < 3, direct, crossed), False)
            return 0

        lax.fori_loop(1, 5, ring_part, 0)
        return 0

    lax.fori_loop(0, CHUNKS, ring_round, 0)

    def far_part(k, _):
        pass_far(k).wait_recv()
        block_part(5, k, 2 * reach * core, False)
        return 0

    lax.fori_loop(0, CHUNKS, far_part, 0)

    total = jnp.zeros((8, LANES), jnp.float32)

    def add_rows(r, total):
        rows = pl.ds(pl.multiple_of(r * LANES, LANES), LANES)
        return total + jnp.sum(row_acc[rows, :].reshape(LANES // 8, 8, LANES), axis=0)

    total = lax.fori_loop(0, n // LANES, add_rows, total)
    e_buf[me] = jnp.broadcast_to(0.5 * jnp.sum(total), (8, LANES))

    def finish(r, _):
        rows = pl.ds(pl.multiple_of(r * LANES, LANES), LANES)
        row_sum = jnp.sum(row_acc[rows, :], axis=1, keepdims=True)
        acc[rows, :] = (row_sum * x_all[0, rows, :].astype(jnp.float32) - acc[rows, :]) * inv_lsq
        return 0

    def out_copy(r):
        rows = pl.ds(pl.multiple_of(r * LANES, LANES), LANES)
        return pltpu.make_async_copy(acc.at[rows], f_hbm.at[rows], out_sem.at[r])

    finish(0, 0)
    energy = [
        pltpu.make_async_remote_copy(
            src_ref=e_buf.at[me], dst_ref=e_buf.at[me], send_sem=esend_sem.at[hop], recv_sem=erecv_sem.at[hop],
            device_id={'seg': lax.rem(me + hop, seg_len)}, device_id_type=MESH)
        for hop in range(1, seg_len)]
    for copy in energy:
        copy.start()

    def finish_and_send(r, _):
        finish(r, 0)
        out_copy(r - 1).start()
        return 0

    lax.fori_loop(1, n // LANES, finish_and_send, 0)
    out_copy(n // LANES - 1).start()

    def drain(k, _):
        for copy in (to_right, to_left, to_mate, pass_left_block, pass_right_block, pass_far):
            copy(k).wait_send()
        return 0

    lax.fori_loop(0, CHUNKS, drain, 0)
    for copy in metas:
        copy.wait_send()
    for copy in energy:
        copy.wait()
    e_sum = e_buf[0]
    for dev in range(1, seg_len):
        e_sum = e_sum + e_buf[dev]
    e_ref[...] = e_sum

    def drain_out(r, _):
        out_copy(r).wait()
        return 0

    lax.fori_loop(0, n // LANES, drain_out, 0)


def solution(mesh):
    seg_len = mesh.shape['seg']

    def device_fn(positions, charges, pair_band):
        n, d = positions.shape
        reach = (pair_band.shape[1] - 1) // 2
        flops = 4 * n * n * d * (2 * reach + 1)
        forces, energy = pl.pallas_call(
            functools.partial(kernel, seg_len, reach),
            out_shape=(jax.ShapeDtypeStruct((n, d), jnp.float32), jax.ShapeDtypeStruct((8, LANES), jnp.float32)),
            in_specs=[pl.BlockSpec(memory_space=pltpu.SMEM), pl.BlockSpec(memory_space=pl.ANY),
                      pl.BlockSpec(memory_space=pltpu.VMEM)],
            out_specs=(pl.BlockSpec(memory_space=pl.ANY), pl.BlockSpec(memory_space=pltpu.VMEM)),
            scratch_shapes=[
                pltpu.VMEM((7, n, d), jnp.bfloat16),
                pltpu.VMEM((7, 2, n), jnp.float32),
                pltpu.VMEM((n, LANES), jnp.float32),
                pltpu.VMEM((n, LANES), jnp.float32),
                pltpu.VMEM((n, d), jnp.float32),
                pltpu.VMEM((n, LANES), jnp.float32),
                pltpu.VMEM((seg_len, 8, LANES), jnp.float32),
                pltpu.SemaphoreType.DMA,
                pltpu.SemaphoreType.DMA((6, CHUNKS)),
                pltpu.SemaphoreType.DMA((7, CHUNKS)),
                pltpu.SemaphoreType.DMA((7,)),
                pltpu.SemaphoreType.DMA((7,)),
                pltpu.SemaphoreType.DMA((seg_len,)),
                pltpu.SemaphoreType.DMA((seg_len,)),
                pltpu.SemaphoreType.DMA((n // LANES,)),
            ],
            compiler_params=pltpu.CompilerParams(
                collective_id=0, has_side_effects=True, vmem_limit_bytes=60 * 2**20),
            cost_estimate=pl.CostEstimate(flops=flops, bytes_accessed=16 * n * d, transcendentals=0),
            name='pair_forces',
        )(pair_band, positions, charges.reshape(1, n))
        return forces, energy[0, 0].reshape(1)

    row_spec = P(('sys', 'seg'), None)
    vec_spec = P(('sys', 'seg'))
    return jax.shard_map(device_fn, mesh=mesh, in_specs=(row_spec, vec_spec, row_spec), out_specs=(row_spec, P('sys')), check_vma=False)
```

time: 613 us -> 217 us (0.35); the launches traced: 604 us -> 217 us
  waiting for transfers between devices: 232 us -> 0 us
  Pallas kernels: 0 us -> 209 us
  starting transfers between devices: 103 us -> 0 us
  blocking collectives: 101 us -> 0 us
  matrix products: 97.9 us -> 0 us
  other arithmetic: 35.2 us -> 0 us
  loops' own time: 12.5 us -> 0 us
  local copies, waits for them, and re-layouts: 18.7 us -> 7.38 us
    ppermute x9 -> x0, waiting for transfers between devices: 232 us -> none  [the longest x3 232 us: device_fn(): q_vis = lax.ppermute(q_vis, 'seg', fwd_perm)]
    pallas_call x0 -> x1, Pallas kernels: none -> 209 us  [device_fn(): pl.pallas_call(functools.partial(kernel, seg_len, reach), out_shape=(jax....]
    ppermute x9 -> x0, starting transfers between devices: 103 us -> none  [the longest x2 98.9 us: device_fn(): react_acc = lax.ppermute(react_acc, 'seg', fwd_perm)]
    psum x1 -> x0, blocking collectives: 101 us -> none  [device_fn(): energy = lax.psum(energy, 'seg')]
    dot_general x5 -> x0, matrix products: 97.9 us -> none  [the longest x2 50.3 us: pair_weights(): jnp.einsum('id,jd->ij', positions, x_vis, preferred_element_type=jnp.floa...]
    add x3 -> x0, other arithmetic: 31.9 us -> none  [the longest x2 18 us: device_fn(): react_acc = react_acc + vis_part]
    another operation x4 -> x0, local copies, waits for them, and re-layouts: 14 us -> none
    another operation x3 -> x0, loops' own time: 12.5 us -> none  [device_fn(): lax.cond(band_row[reach_steps - step_idx] != 0, live_pair, dead_pair, (x_...]
  transfers between devices with their start and end apart: 9 -> 0, of which waited for: 3 -> 0; matrix products, arithmetic and copies ran while one was open for 18% -> 0% of each run, Pallas kernels for 0% -> 0%
where the time goes in v1:
time: 217 us
  Pallas kernels  209 us (96%)
  local copies, waits for them, and re-layouts  7.38 us (3%)
    pallas_call x1, Pallas kernels, device_fn(): pl.pallas_call(functools.partial(kernel, seg_len, reach), out_shape=(jax....  209 us
    unnamed x1, local copies, waits for them, and re-layouts  6.2 us

profile of v1, /device:TPU:81, one launch (start us, length us, event | category | flops | bytes accessed | tf_op | source)
XLA Modules:
  0.0 216.7 jit_solution(11039342738913340520)
XLA Ops:
  0.6 208.7 %pair_forces.1 = (f32[3072,512]{1,0:T(8,128)}, f32[8,128]{1,0:T(8,128)}) custom-call(s32[1,7]{1,0:T(1,128)} %band_ref.1, bf16[3072,512]{1,0:T(8,128)(2,1)} %x_hbm.1, f32[1,3072]{1,0:T(1,128)} %bitcast.2), custom_call_target="tpu_custom_call" | custom-call | flops 135291469824 | bytes 25165824 | tf_op jit(solution)/shard_map/pair_forces/pallas_call | solution.py:244
  209.3 1.2 slice.3
  210.5 6.2 %copy.6 = f32[3072,512]{1,0:T(8,128)} copy(f32[3072,512]{1,0:T(8,128)} %get-tuple-element.8) | data formatting | bytes 12582912

commit v2 on v1

--- a/solution.py
+++ b/solution.py
@@ -11,10 +11,11 @@
 MESH = pl.DeviceIdType.MESH
 LANES = 128
 CHUNKS = 6
-ROW_TILE = 1024
-
-
-def kernel(seg_len, reach, band_ref, x_hbm, q_ref, f_hbm, e_ref, x_all, meta, a_col, q_col, acc, row_acc, e_buf,
+TILE = 256
+PIECE = 64
+
+
+def kernel(seg_len, reach, band_ref, x_hbm, q_ref, f_hbm, e_ref, x_all, meta, a_col, q_col, acc, row_acc, s_buf, w_buf, diag, e_buf,
            local_sem, send_sem, recv_sem, msend_sem, mrecv_sem, esend_sem, erecv_sem, out_sem):
     n, d = x_hbm.shape
     chunk = n // CHUNKS
@@ -91,6 +92,8 @@
         for slot, dev in peers]
     for copy in metas:
         copy.start()
+    columns = {1: reach - 2, 2: reach + 2, 3: reach - 1 - 2 * core, 4: reach + 3 - 2 * core, 5: 2 * reach * core,
+               6: reach + 1 - 2 * core}
 
     def start_rest(k, _):
         to_right(k).start()
@@ -100,32 +103,12 @@
 
     lax.fori_loop(1, CHUNKS, start_rest, 0)
 
-    def block_part(slot, k, column, own):
-        cols = pl.ds(pl.multiple_of(k * chunk, chunk), chunk)
-        live = band_ref[0, column] != 0
-        q_row = jnp.where(live, meta[slot, 0:1, cols], 0.0)
-        b_row = meta[slot, 1:2, cols]
-
-        def row_tile(i, _):
-            rows = pl.ds(pl.multiple_of(i * ROW_TILE, ROW_TILE), ROW_TILE)
-            x_vis = x_all[slot, cols, :]
-            dots = lax.dot_general(x_all[0, rows, :], x_vis, (((1,), (1,)), ((), ())),
-                                   preferred_element_type=jnp.float32)
-            a_tile = jnp.concatenate([a_col[rows, :]] * (chunk // LANES), axis=1)
-            q_tile = jnp.concatenate([q_col[rows, :]] * (chunk // LANES), axis=1)
-            weights = jnp.exp2(jnp.minimum((dots * (2.0 * scale) + a_tile) + b_row, 0.0)) * q_row * q_tile
-            if own:
-                row_id = lax.broadcasted_iota(jnp.int32, weights.shape, 0) + i * ROW_TILE
-                col_id = lax.broadcasted_iota(jnp.int32, weights.shape, 1) + k * chunk
-                weights = jnp.where(row_id == col_id, 0.0, weights)
-            part = weights[:, 0:LANES]
-            for s in range(1, chunk // LANES):
-                part = part + weights[:, s * LANES:(s + 1) * LANES]
-            row_acc[rows, :] += part
-            acc[rows, :] += jnp.dot(weights.astype(jnp.bfloat16), x_vis, preferred_element_type=jnp.float32)
-            return 0
-
-        lax.fori_loop(0, n // ROW_TILE, row_tile, 0)
+    meta[7] = jnp.zeros((2, n), jnp.float32)
+    row_id = lax.broadcasted_iota(jnp.int32, (TILE, 2 * TILE), 0)
+    col_id = lax.broadcasted_iota(jnp.int32, (TILE, 2 * TILE), 1)
+    for half in range(2):
+        diag[half] = jnp.where(row_id + half * TILE == col_id, -1e30, 0.0)
+    diag[2] = jnp.zeros((TILE, 2 * TILE), jnp.float32)
 
     def serve(k):
         to_right(k).wait_recv()
@@ -134,47 +117,108 @@
         pass_right_block(k).start()
         pass_far(k).start()
 
-    def own_part(k, _):
-        block_part(0, k, reach, True)
-        return 0
-
-    lax.fori_loop(0, CHUNKS, own_part, 0)
-    serve(0)
-    for copy in metas:
-        copy.wait_recv()
-
-    def mate_part(k, _):
-        to_mate(k).wait_recv()
-        block_part(6, k, reach + 1 - 2 * core, False)
-        return 0
-
-    lax.fori_loop(0, CHUNKS, mate_part, 0)
-
-    def ring_round(k, _):
-        @pl.when(k + 1 < CHUNKS)
+    tiles = n // TILE
+    ring = 2 * CHUNKS
+    last = ring + 4 * CHUNKS
+
+    def place(task):
+        turn = task - ring
+        slot = jnp.where(task < CHUNKS, 0, jnp.where(task < ring, 6, jnp.where(task < last, 1 + lax.rem(turn, 4), 5)))
+        k = jnp.where(task < CHUNKS, CHUNKS - 1 - task,
+                      jnp.where(task < ring, task - CHUNKS, jnp.where(task < last, turn // 4, task - last)))
+        return slot, k
+
+    def block(slot, k):
+        return x_all[slot, pl.ds(pl.multiple_of(k * chunk, chunk), chunk), :]
+
+    def dots(i, slot, k):
+        return lax.dot_general(x_all[0, i * TILE:(i + 1) * TILE, :], block(slot, k), (((1,), (1,)), ((), ())),
+                               preferred_element_type=jnp.float32)
+
+    def weigh(dot_tile, i, slot, k, buf, cap):
+        for p in range(TILE // PIECE):
+            rows = slice(i * TILE + p * PIECE, i * TILE + (p + 1) * PIECE)
+            tile_rows = slice(p * PIECE, (p + 1) * PIECE)
+            a_piece = a_col[rows, :]
+            q_piece = q_col[rows, :]
+            part = row_acc[rows, :]
+            for h in range(chunk // LANES):
+                lanes = slice(h * LANES, (h + 1) * LANES)
+                cols = pl.ds(pl.multiple_of(k * chunk + h * LANES, LANES), LANES)
+                power = (dot_tile[tile_rows, lanes] * (2.0 * scale) + a_piece) + meta[slot, 1:2, cols]
+                power = jnp.minimum(power, 0.0 if cap is None else diag[cap, tile_rows, lanes])
+                w = jnp.exp2(power) * meta[slot, 0:1, cols] * q_piece
+                part = part + w
+                w_buf[buf, tile_rows, lanes] = w.astype(jnp.bfloat16)
+            row_acc[rows, :] = part
+
+    def pull(i, slot, k, buf):
+        acc[i * TILE:(i + 1) * TILE, :] += jnp.dot(w_buf[buf], block(slot, k), preferred_element_type=jnp.float32)
+
+    def run_task(task, own):
+        slot, k = place(task)
+        was_slot, was_k = place(jnp.maximum(task - 1, 0))
+        was_meta = jnp.where(task == 0, 7, was_slot)
+        held = s_buf[...]
+        for i in range(tiles):
+            i1, slot1, k1, meta1 = (tiles - 1, was_slot, was_k, was_meta) if i == 0 else (i - 1, slot, k, slot)
+            cap = None
+            if own:
+                step = i1 - 2 * k1
+                cap = jnp.where((step == 0) | (step == 1), step, 2)
+            fresh = dots(i, slot, k)
+            weigh(held, i1, meta1, k1, i % 2, cap)
+            pull(i1, slot1, k1, i % 2)
+            held = fresh
+        s_buf[...] = held
+
+    s_buf[...] = jnp.zeros(s_buf.shape, jnp.float32)
+
+    def own_task(task, _):
+        @pl.when(task == CHUNKS - 1)
         def _():
-            serve(k + 1)
-
-        pass_left_block(k).wait_recv()
-        pass_right_block(k).wait_recv()
-
-        def ring_part(slot, _):
-            direct = jnp.where(slot == 1, reach - 2, reach + 2)
-            crossed = jnp.where(slot == 3, reach - 1 - 2 * core, reach + 3 - 2 * core)
-            block_part(slot, k, jnp.where(slot < 3, direct, crossed), False)
-            return 0
-
-        lax.fori_loop(1, 5, ring_part, 0)
-        return 0
-
-    lax.fori_loop(0, CHUNKS, ring_round, 0)
-
-    def far_part(k, _):
-        pass_far(k).wait_recv()
-        block_part(5, k, 2 * reach * core, False)
-        return 0
-
-    lax.fori_loop(0, CHUNKS, far_part, 0)
+            for copy in metas:
+                copy.wait_recv()
+            for s, column in columns.items():
+                meta[s, 0:1, :] = jnp.where(band_ref[0, column] != 0, meta[s, 0:1, :], 0.0)
+
+            def wait_mate(k, _):
+                to_mate(k).wait_recv()
+                return 0
+
+            lax.fori_loop(0, CHUNKS, wait_mate, 0)
+            serve(0)
+
+        run_task(task, True)
+        return 0
+
+    lax.fori_loop(0, CHUNKS, own_task, 0)
+
+    def other_task(task, _):
+        coming = task + 1 - ring
+        k = coming // 4
+
+        @pl.when((coming >= 0) & (lax.rem(coming, 4) == 0) & (k < CHUNKS))
+        def _():
+            pass_left_block(k).wait_recv()
+            pass_right_block(k).wait_recv()
+
+            @pl.when(k + 1 < CHUNKS)
+            def _():
+                serve(k + 1)
+
+        @pl.when((task + 1 >= last) & (task + 1 < last + CHUNKS))
+        def _():
+            pass_far(task + 1 - last).wait_recv()
+
+        run_task(task, False)
+        return 0
+
+    lax.fori_loop(CHUNKS, last + CHUNKS, other_task, 0)
+
+    slot, k = place(last + CHUNKS - 1)
+    weigh(s_buf[...], tiles - 1, slot, k, 0, None)
+    pull(tiles - 1, slot, k, 0)
 
     total = jnp.zeros((8, LANES), jnp.float32)
 
@@ -249,11 +293,14 @@
             out_specs=(pl.BlockSpec(memory_space=pl.ANY), pl.BlockSpec(memory_space=pltpu.VMEM)),
             scratch_shapes=[
                 pltpu.VMEM((7, n, d), jnp.bfloat16),
-                pltpu.VMEM((7, 2, n), jnp.float32),
+                pltpu.VMEM((8, 2, n), jnp.float32),
                 pltpu.VMEM((n, LANES), jnp.float32),
                 pltpu.VMEM((n, LANES), jnp.float32),
                 pltpu.VMEM((n, d), jnp.float32),
                 pltpu.VMEM((n, LANES), jnp.float32),
+                pltpu.VMEM((TILE, 2 * TILE), jnp.float32),
+                pltpu.VMEM((2, TILE, 2 * TILE), jnp.bfloat16),
+                pltpu.VMEM((3, TILE, 2 * TILE), jnp.float32),
                 pltpu.VMEM((seg_len, 8, LANES), jnp.float32),
                 pltpu.SemaphoreType.DMA,
                 pltpu.SemaphoreType.DMA((6, CHUNKS)),

time: 217 us -> 202 us (0.931)
  Pallas kernels: 209 us -> 193 us
    pallas_call x1, Pallas kernels: 209 us -> 193 us  [device_fn(): pl.pallas_call(functools.partial(kernel, seg_len, reach), out_shape=(jax....]
where the time goes in v2:
time: 202 us; the launch traced here: 201 us
  Pallas kernels  193 us (96%)
  local copies, waits for them, and re-layouts  7.38 us (4%)
    pallas_call x1, Pallas kernels, device_fn(): pl.pallas_call(functools.partial(kernel, seg_len, reach), out_shape=(jax....  193 us
    unnamed x1, local copies, waits for them, and re-layouts  6.2 us

profile of v2, /device:TPU:81, one launch (start us, length us, event | category | flops | bytes accessed | tf_op | source)
XLA Modules:
  0.0 201.5 jit_solution(4742130278873779647)
XLA Ops:
  0.6 193.5 %pair_forces.1 = (f32[3072,512]{1,0:T(8,128)}, f32[8,128]{1,0:T(8,128)}) custom-call(s32[1,7]{1,0:T(1,128)} %band_ref.1, bf16[3072,512]{1,0:T(8,128)(2,1)} %x_hbm.1, f32[1,3072]{1,0:T(1,128)} %bitcast.2), custom_call_target="tpu_custom_call" | custom-call | flops 135291469824 | bytes 25165824 | tf_op jit(solution)/shard_map/pair_forces/pallas_call | solution.py:288
  194.1 1.2 slice.3
  195.3 6.2 %copy.6 = f32[3072,512]{1,0:T(8,128)} copy(f32[3072,512]{1,0:T(8,128)} %get-tuple-element.8) | data formatting | bytes 12582912

commit v3 on v2

v3 whole, which is shorter than its diff:
```python
import functools
import math

import jax
import jax.numpy as jnp
from jax import lax
from jax.experimental import pallas as pl
from jax.experimental.pallas import tpu as pltpu
from jax.sharding import PartitionSpec as P

MESH = pl.DeviceIdType.MESH
LANES = 128
CHUNKS = 6
TILE = 256
PIECE = 64
PIECES = TILE // PIECE
UNROLL = 2
SERVE = (0, 8, 10, 13, 15)


def gather_kernel(seg_len, reach, band_ref, x_hbm, q_ref, acc_hbm, row_hbm, a_hbm, q_hbm, meta_hbm, left_hbm, right_hbm,
                  left_x_hbm, right_x_hbm, x_flat, meta, a_col, q_col, acc, row_acc, s_buf, w_buf, diag,
                  local_sem, first_sem, send_sem, recv_sem, msend_sem, mrecv_sem, out_sem):
    n, d = x_hbm.shape
    chunk = n // CHUNKS
    me = lax.axis_index('seg')
    core = lax.rem(me, 2)
    mate = me + 1 - 2 * core
    right = lax.rem(me + 2, seg_len)
    left = lax.rem(me + seg_len - 2, seg_len)
    right_x = right + 1 - 2 * core
    left_x = left + 1 - 2 * core
    far_x = lax.rem(me + 4, seg_len) + 1 - 2 * core
    scale = math.log2(math.e) * 0.5 / d
    inv_lsq = 1.0 / d

    load = pltpu.make_async_copy(x_hbm, x_flat.at[pl.ds(0, n)], local_sem)
    load.start()

    barrier = pltpu.get_barrier_semaphore()
    for hop in range(1, seg_len):
        pl.semaphore_signal(barrier, inc=1, device_id={'seg': lax.rem(me + hop, seg_len)}, device_id_type=MESH)
    pl.semaphore_wait(barrier, seg_len - 1)

    landing = {1: left_hbm, 2: right_hbm, 3: left_x_hbm, 4: right_x_hbm, 6: x_flat.at[pl.ds(n, n)]}

    def send(kind, k, src, slot, dev):
        rows = pl.ds(pl.multiple_of(k * chunk, chunk), chunk)
        return pltpu.make_async_remote_copy(
            src_ref=src.at[rows], dst_ref=landing[slot].at[rows], send_sem=send_sem.at[kind, k],
            recv_sem=recv_sem.at[slot, k], device_id={'seg': dev}, device_id_type=MESH)

    def to_right(k):
        return send(0, k, x_hbm, 1, right)

    def to_left(k):
        return send(1, k, x_hbm, 2, left)

    def to_mate(k):
        return send(2, k, x_hbm, 6, mate)

    def pass_left_block(k):
        return send(3, k, left_hbm, 3, mate)

    def pass_right_block(k):
        return send(4, k, right_hbm, 4, mate)

    to_right(0).start()
    to_left(0).start()
    load.wait()

    def prologue(r, _):
        rows = pl.ds(pl.multiple_of(r * LANES, LANES), LANES)
        x = x_flat[rows, :].astype(jnp.float32)
        neg = jnp.sum(x * x, axis=1, keepdims=True) * (-scale)
        neg = jnp.broadcast_to(neg, (LANES, LANES))
        a_col[rows, :] = neg
        q_row = q_ref[:, rows]
        meta[0, 1:2, rows] = neg.T[0:1, :]
        meta[0, 0:1, rows] = q_row
        q_col[rows, :] = jnp.broadcast_to(q_row, (LANES, LANES)).T
        row_acc[rows, :] = jnp.zeros((LANES, LANES), jnp.float32)
        acc[rows, :] = jnp.zeros((LANES, d), jnp.float32)
        return 0

    lax.fori_loop(0, n // LANES, prologue, 0)

    to_mate(0).start()
    peers = ((1, right), (2, left), (3, right_x), (4, left_x), (5, far_x), (6, mate))
    metas = [
        pltpu.make_async_remote_copy(
            src_ref=meta.at[0], dst_ref=meta.at[slot], send_sem=msend_sem.at[slot], recv_sem=mrecv_sem.at[slot],
            device_id={'seg': dev}, device_id_type=MESH)
        for slot, dev in peers]
    for copy in metas:
        copy.start()
    columns = {1: reach - 2, 2: reach + 2, 3: reach - 1 - 2 * core, 4: reach + 3 - 2 * core, 5: 2 * reach * core,
               6: reach + 1 - 2 * core}

    def start_rest(k, _):
        to_right(k).start()
        to_left(k).start()
        to_mate(k).start()
        return 0

    lax.fori_loop(1, CHUNKS, start_rest, 0)

    meta[7] = jnp.zeros((2, n), jnp.float32)
    row_id = lax.broadcasted_iota(jnp.int32, (TILE, 2 * TILE), 0)
    col_id = lax.broadcasted_iota(jnp.int32, (TILE, 2 * TILE), 1)
    for half in range(2):
        diag[half] = jnp.where(row_id + half * TILE == col_id, -1e30, 0.0)
    diag[2] = jnp.zeros((TILE, 2 * TILE), jnp.float32)

    def serve(k):
        to_right(k).wait_recv()
        to_left(k).wait_recv()
        pass_left_block(k).start()
        pass_right_block(k).start()

    tiles = n // TILE
    ring = 2 * CHUNKS
    last = ring + 4

    def place(task):
        slot = jnp.where(task < CHUNKS, 0, jnp.where(task < ring, 6, 1 + task - ring))
        k = jnp.where(task < CHUNKS, CHUNKS - 1 - task, jnp.where(task < ring, task - CHUNKS, 0))
        return slot, k

    def block(task):
        slot, k = place(task)
        row = jnp.where(task < ring, jnp.where(slot == 0, 0, n) + k * chunk, 2 * n + (task - ring) * chunk)
        return x_flat[pl.ds(pl.multiple_of(row, chunk), chunk), :]

    def dots(i, task):
        return lax.dot_general(x_flat[i * TILE:(i + 1) * TILE, :], block(task), (((1,), (1,)), ((), ())),
                               preferred_element_type=jnp.float32)

    def weigh(dot_tile, i, slot, k, buf, cap):
        for p in range(TILE // PIECE):
            rows = slice(i * TILE + p * PIECE, i * TILE + (p + 1) * PIECE)
            tile_rows = slice(p * PIECE, (p + 1) * PIECE)
            a_piece = a_col[rows, :]
            q_piece = q_col[rows, :]
            part = row_acc[rows, :]
            for h in range(chunk // LANES):
                lanes = slice(h * LANES, (h + 1) * LANES)
                cols = pl.ds(pl.multiple_of(k * chunk + h * LANES, LANES), LANES)
                power = (dot_tile[tile_rows, lanes] * (2.0 * scale) + a_piece) + meta[slot, 1:2, cols]
                power = jnp.minimum(power, 0.0 if cap is None else diag[cap, tile_rows, lanes])
                w = jnp.exp2(power) * meta[slot, 0:1, cols] * q_piece
                part = part + w
                w_buf[buf, tile_rows, lanes] = w.astype(jnp.bfloat16)
            row_acc[rows, :] = part

    def pull(i, task, buf):
        acc[i * TILE:(i + 1) * TILE, :] += jnp.dot(w_buf[buf], block(task), preferred_element_type=jnp.float32)

    def run_task(task, own):
        slot, k = place(task)
        was = jnp.maximum(task - 1, 0)
        was_slot, was_k = place(was)
        was_meta = jnp.where(task == 0, 7, was_slot)
        held = s_buf[...]
        for i in range(tiles):
            i1, task1, k1, meta1 = (tiles - 1, was, was_k, was_meta) if i == 0 else (i - 1, task, k, slot)
            cap = None
            if own:
                step = i1 - 2 * k1
                cap = jnp.where((step == 0) | (step == 1), step, 2)
            fresh = dots(i, task)
            weigh(held, i1, meta1, k1, i % 2, cap)
            pull(i1, task1, i % 2)
            held = fresh
        s_buf[...] = held

    s_buf[...] = jnp.zeros(s_buf.shape, jnp.float32)

    def own_task(task, _):
        @pl.when(task == CHUNKS - 1)
        def _():
            for copy in metas:
                copy.wait_recv()
            for s, column in columns.items():
                meta[s, 0:1, :] = jnp.where(band_ref[0, column] != 0, meta[s, 0:1, :], 0.0)

            def wait_mate(k, _):
                to_mate(k).wait_recv()
                return 0

            lax.fori_loop(0, CHUNKS, wait_mate, 0)
            serve(0)

        run_task(task, True)
        return 0

    lax.fori_loop(0, CHUNKS, own_task, 0)

    firsts = [
        pltpu.make_async_copy(landing[slot].at[pl.ds(0, chunk)],
                              x_flat.at[pl.ds(2 * n + (slot - 1) * chunk, chunk)], first_sem.at[slot])
        for slot in range(1, 5)]

    def other_task(task, _):
        @pl.when(task == ring - 2)
        def _():
            pass_left_block(0).wait_recv()
            pass_right_block(0).wait_recv()
            for copy in firsts:
                copy.start()

        @pl.when(task == ring - 1)
        def _():
            for copy in firsts:
                copy.wait()

        for k in range(1, CHUNKS - 1):
            @pl.when(task == SERVE[k])
            def _(k=k):
                serve(k)

        run_task(task, False)
        return 0

    lax.fori_loop(CHUNKS, last, other_task, 0)

    slot, k = place(last - 1)
    weigh(s_buf[...], tiles - 1, slot, k, 0, None)
    pull(tiles - 1, last - 1, 0)

    outs = [pltpu.make_async_copy(src, dst, out_sem.at[j])
            for j, (src, dst) in enumerate(((acc, acc_hbm), (row_acc, row_hbm), (a_col, a_hbm), (q_col, q_hbm), (meta, meta_hbm)))]
    for copy in outs:
        copy.start()
    serve(CHUNKS - 1)

    def drain(k, _):
        for copy in (to_right, to_left, to_mate, pass_left_block, pass_right_block):
            copy(k).wait_send()
        return 0

    def arrive(k, _):
        pass_left_block(k).wait_recv()
        pass_right_block(k).wait_recv()
        return 0

    lax.fori_loop(0, CHUNKS, drain, 0)
    lax.fori_loop(1, CHUNKS, arrive, 0)
    for copy in metas:
        copy.wait_send()
    for copy in outs:
        copy.wait()


def pair_kernel(parts, final, meta_rows, band_ref, x_hbm, a_hbm, q_hbm, *refs):
    n, d = x_hbm.shape
    n_src = len(parts)
    sources, refs = refs[:n_src], refs[n_src:]
    meta_hbm, refs = refs[0], refs[1:]
    if final:
        acc_old, row_old, acc_new, row_new, f_hbm, e_ref = refs[:6]
        (x_own, vis, meta, meta_all, a_col, q_col, acc, row_acc, w_buf, acc_in, row_in, load_sem, vis_sem, old_sem,
         out_sem) = refs[6:]
    else:
        acc_hbm, row_hbm = refs[:2]
        x_own, vis, meta, meta_all, a_col, q_col, acc, row_acc, w_buf, load_sem, vis_sem, out_sem = refs[2:]
    chunk = n // CHUNKS
    tasks = sum(count for _, _, count, _, _ in parts)
    tiles = n // TILE
    core = lax.rem(lax.axis_index('seg'), 2)
    scale = math.log2(math.e) * 0.5 / d

    def fetch(source, k, task):
        return pltpu.make_async_copy(source.at[pl.ds(k * chunk, chunk)], vis.at[pl.ds(task * chunk, chunk)],
                                     vis_sem.at[task])

    plan = []
    for source, (want, first, count, slot, column) in zip(sources, parts):
        plan += [(source, want, first + j, slot, column) for j in range(count)]
    plan_tasks = meta_rows(plan)

    def start_fetch(task):
        for source, want, k in plan_tasks[task][0]:
            if want is None:
                fetch(source, k, task).start()
            else:
                @pl.when(core == want)
                def _():
                    fetch(source, k, task).start()

    loads = [pltpu.make_async_copy(src, dst, load_sem.at[j])
             for j, (src, dst) in enumerate(((meta_hbm, meta_all), (x_hbm, x_own), (a_hbm, a_col), (q_hbm, q_col)))]
    n_tasks = len(plan_tasks)
    start_fetch(0)
    for copy in loads:
        copy.start()
    for task in range(1, n_tasks):
        start_fetch(task)
    if final:
        olds = [pltpu.make_async_copy(src, dst, old_sem.at[j])
                for j, (src, dst) in enumerate(((acc_old, acc_in.at[0]), (acc_new, acc_in.at[1]),
                                                (row_old, row_in.at[0]), (row_new, row_in.at[1])))]
        for copy in olds:
            copy.start()

    def clear(r, _):
        rows = pl.ds(pl.multiple_of(r * LANES, LANES), LANES)
        acc[rows, :] = jnp.zeros((LANES, d), jnp.float32)
        row_acc[rows, :] = jnp.zeros((LANES, LANES), jnp.float32)
        return 0

    lax.fori_loop(0, n // LANES, clear, 0)
    w_buf[...] = jnp.zeros(w_buf.shape, jnp.bfloat16)
    for copy in loads:
        copy.wait()
    for task in range(n_tasks):
        _, k, slot, column = plan_tasks[task]
        cols = slice(task * chunk, (task + 1) * chunk)
        own_cols = slice(k * chunk, (k + 1) * chunk)
        meta[0:1, cols] = jnp.where(band_ref[0, column(core)] != 0, meta_all[slot, 0:1, own_cols], 0.0)
        meta[1:2, cols] = meta_all[slot, 1:2, own_cols]
    meta[:, n_tasks * chunk:(n_tasks + 1) * chunk] = jnp.zeros((2, chunk), jnp.float32)

    def arrived(task):
        fetch(sources[0], 0, task).wait()

    def product(acc1, acc2):
        def push(task, rows_half, cols_half, register, mxu, transpose):
            rows = pl.ds(pl.multiple_of(task * chunk + rows_half * TILE, TILE), TILE)
            tile = vis[rows, cols_half * TILE:(cols_half + 1) * TILE]
            pltpu.matmul_push_rhs(tile, register, mxu, transpose=transpose)

        def push_dots(task, half):
            for mxu in range(2):
                push(task, mxu, half, half, mxu, True)

        def push_pull(task, half):
            for mxu in range(2):
                push(task, half, mxu, half, mxu, False)

        def piece_rows(i, p):
            return pl.ds(pl.multiple_of(i * TILE + p * PIECE, PIECE), PIECE)

        def dots(i, buf, half):
            for p in range(PIECES):
                lhs = x_own[piece_rows(i, p), half * TILE:(half + 1) * TILE]
                for mxu in range(2):
                    pltpu.matmul_acc_lhs(acc1[buf][mxu][p], lhs, load_staged_rhs=half if p == 0 else None)

        def pull(buf, half):
            for p in range(PIECES):
                lhs = w_buf[buf, p * PIECE:(p + 1) * PIECE, half * TILE:(half + 1) * TILE]
                for mxu in range(2):
                    pltpu.matmul_acc_lhs(acc2[mxu][p], lhs, load_staged_rhs=half if p == 0 else None)

        def weigh(i, task, buf, mxu):
            for p in range(PIECES):
                rows = piece_rows(i, p)
                dot_piece = pltpu.matmul_pop(acc1[buf][mxu][p])
                a_piece = a_col[rows, :]
                q_piece = q_col[rows, :]
                part = row_acc[rows, :]
                for h in range(TILE // LANES):
                    first = mxu * TILE + h * LANES
                    cols = pl.ds(pl.multiple_of(task * chunk + first, LANES), LANES)
                    power = (dot_piece[:, h * LANES:(h + 1) * LANES] * (2.0 * scale) + a_piece) + meta[1:2, cols]
                    power = jnp.minimum(power, 0.0)
                    w = jnp.exp2(power) * meta[0:1, cols] * q_piece
                    part = part + w
                    w_buf[buf, p * PIECE:(p + 1) * PIECE, first:first + LANES] = w.astype(jnp.bfloat16)
                row_acc[rows, :] = part

        def take_pull(i):
            for p in range(PIECES):
                rows = piece_rows(i, p)
                for mxu in range(2):
                    acc[rows, mxu * TILE:(mxu + 1) * TILE] += pltpu.matmul_pop(acc2[mxu][p])

        def run_task(task, _):
            was = jnp.maximum(task - 1, 0)
            was_meta = jnp.where(task == 0, n_tasks, was)
            coming = jnp.minimum(task + 1, n_tasks - 1)

            @pl.when(task + 1 < n_tasks)
            def _():
                arrived(task + 1)

            def body(g, _):
                for u in range(UNROLL):
                    i = g * UNROLL + u
                    buf = u % 2
                    task1, meta1, task3 = task, task, task
                    if u == 0:
                        i1, i2 = lax.rem(i + tiles - 1, tiles), lax.rem(i + tiles - 2, tiles)
                        task1, meta1 = jnp.where(g == 0, was, task), jnp.where(g == 0, was_meta, task)
                    else:
                        i1 = i - 1
                        i2 = lax.rem(i + tiles - 2, tiles) if u == 1 else i - 2
                    if u == UNROLL - 1:
                        task3 = jnp.where(g == tiles // UNROLL - 1, coming, task)
                    dots(i, buf, 0)
                    push_pull(task1, 0)
                    weigh(i1, meta1, 1 - buf, 0)
                    dots(i, buf, 1)
                    push_pull(task1, 1)
                    take_pull(i2)
                    weigh(i1, meta1, 1 - buf, 1)
                    pull(1 - buf, 0)
                    push_dots(task3, 0)
                    pull(1 - buf, 1)
                    push_dots(task3, 1)
                return 0

            lax.fori_loop(0, tiles // UNROLL, body, 0)
            return 0

        for refs in acc1[0] + acc1[1] + acc2:
            for ref in refs:
                pltpu.matmul_pop(ref)
        arrived(0)
        push_dots(0, 0)
        push_dots(0, 1)
        lax.fori_loop(0, n_tasks, run_task, 0)

        spare = x_own[0:PIECE, 0:TILE]
        for half in range(2):
            for mxu in range(2):
                pltpu.matmul_acc_lhs(acc1[0][mxu][0], spare, load_staged_rhs=half)
            push_pull(n_tasks - 1, half)
        for mxu in range(2):
            pltpu.matmul_pop(acc1[0][mxu][0])
        take_pull(tiles - 2)
        weigh(tiles - 1, n_tasks - 1, 1, 0)
        weigh(tiles - 1, n_tasks - 1, 1, 1)
        pull(1, 0)
        pull(1, 1)
        take_pull(tiles - 1)

    piece = [[pltpu.ACC(mxu)((PIECE, TILE), jnp.float32) for _ in range(PIECES)] for mxu in range(2)]
    pl.run_scoped(product, (piece, piece), piece)

    if not final:
        outs = [pltpu.make_async_copy(src, dst, out_sem.at[j])
                for j, (src, dst) in enumerate(((acc, acc_hbm), (row_acc, row_hbm)))]
        for copy in outs:
            copy.start()
        for copy in outs:
            copy.wait()
        return

    for copy in olds:
        copy.wait()

    def out_copy(r):
        rows = pl.ds(pl.multiple_of(r * LANES, LANES), LANES)
        return pltpu.make_async_copy(acc.at[rows], f_hbm.at[rows], out_sem.at[r])

    def finish(r, total):
        rows = pl.ds(pl.multiple_of(r * LANES, LANES), LANES)
        row_parts = row_acc[rows, :] + (row_in[0, rows, :] + row_in[1, rows, :])
        row_sum = jnp.sum(row_parts, axis=1, keepdims=True)
        pulls = acc[rows, :] + (acc_in[0, rows, :] + acc_in[1, rows, :])
        acc[rows, :] = (row_sum * x_own[rows, :].astype(jnp.float32) - pulls) * (1.0 / d)
        out_copy(r).start()
        return total + jnp.sum(row_parts.reshape(LANES // 8, 8, LANES), axis=0)

    total = lax.fori_loop(0, n // LANES, finish, jnp.zeros((8, LANES), jnp.float32))
    e_ref[...] = jnp.broadcast_to(0.5 * jnp.sum(total), (8, LANES))

    def drain_out(r, _):
        out_copy(r).wait()
        return 0

    lax.fori_loop(0, n // LANES, drain_out, 0)


def by_task(plan):
    tasks, twins = [], {}
    for source, want, k, slot, column in plan:
        if want is not None and (slot, k) in twins:
            tasks[twins[slot, k]][0].append((source, want, k))
            continue
        twins[slot, k] = len(tasks)
        tasks.append(([(source, want, k)], k, slot, column))
    return tasks


def energy_kernel(seg_len, e_in, e_ref, e_buf, esend_sem, erecv_sem):
    me = lax.axis_index('seg')
    e_buf[me] = e_in[...]
    barrier = pltpu.get_barrier_semaphore()
    for hop in range(1, seg_len):
        pl.semaphore_signal(barrier, inc=1, device_id={'seg': lax.rem(me + hop, seg_len)}, device_id_type=MESH)
    pl.semaphore_wait(barrier, seg_len - 1)
    energy = [
        pltpu.make_async_remote_copy(
            src_ref=e_in, dst_ref=e_buf.at[me], send_sem=esend_sem.at[hop], recv_sem=erecv_sem.at[hop],
            device_id={'seg': lax.rem(me + hop, seg_len)}, device_id_type=MESH)
        for hop in range(1, seg_len)]
    for copy in energy:
        copy.start()
    for copy in energy:
        copy.wait()
    e_sum = e_buf[0]
    for dev in range(1, seg_len):
        e_sum = e_sum + e_buf[dev]
    e_ref[...] = e_sum


def solution(mesh):
    seg_len = mesh.shape['seg']

    def device_fn(positions, charges, pair_band):
        n, d = positions.shape
        reach = (pair_band.shape[1] - 1) // 2
        chunk = n // CHUNKS
        hbm, vmem, smem = (pl.BlockSpec(memory_space=m) for m in (pl.ANY, pltpu.VMEM, pltpu.SMEM))
        f32, bf16, dma = jnp.float32, jnp.bfloat16, pltpu.SemaphoreType.DMA
        sums = (jax.ShapeDtypeStruct((n, d), f32), jax.ShapeDtypeStruct((n, LANES), f32))
        cols = (jax.ShapeDtypeStruct((n, LANES), f32),) * 2
        block = jax.ShapeDtypeStruct((n, d), bf16)

        def cost(chunks):
            return pl.CostEstimate(flops=4 * n * chunk * d * chunks, bytes_accessed=16 * n * d, transcendentals=0)

        acc_a, row_a, a_col, q_col, meta, left, right, left_x, right_x = pl.pallas_call(
            functools.partial(gather_kernel, seg_len, reach),
            out_shape=sums + cols + (jax.ShapeDtypeStruct((8, 2, n), f32),) + (block,) * 4,
            in_specs=[smem, hbm, vmem],
            out_specs=(hbm,) * 9,
            scratch_shapes=[
                pltpu.VMEM((2 * n + 4 * chunk, d), bf16),
                pltpu.VMEM((8, 2, n), f32),
                pltpu.VMEM((n, LANES), f32),
                pltpu.VMEM((n, LANES), f32),
                pltpu.VMEM((n, d), f32),
                pltpu.VMEM((n, LANES), f32),
                pltpu.VMEM((TILE, chunk), f32),
                pltpu.VMEM((2, TILE, chunk), bf16),
                pltpu.VMEM((3, TILE, chunk), f32),
                dma, dma((5,)), dma((5, CHUNKS)), dma((7, CHUNKS)), dma((7,)), dma((7,)), dma((5,)),
            ],
            compiler_params=pltpu.CompilerParams(
                collective_id=0, has_side_effects=True, vmem_limit_bytes=60 * 2**20),
            cost_estimate=cost(2 * CHUNKS + 4),
            name='gather_pairs',
        )(pair_band, positions, charges.reshape(1, n))

        ups = [(dev, (dev + 1) % seg_len) for dev in range(1, seg_len, 2)]
        downs = [(dev, (dev - 1) % seg_len) for dev in range(0, seg_len, 2)]
        far_up = lax.ppermute(left, 'seg', ups)
        far_down = lax.ppermute(right, 'seg', downs)

        def pairs(parts, sources, old):
            final = old is not None
            count = len({(slot, first + j) for want, first, number, slot, _ in parts for j in range(number)})
            scratch = [
                pltpu.VMEM((n, d), bf16), pltpu.VMEM((count * chunk, d), bf16), pltpu.VMEM((2, (count + 1) * chunk), f32),
                pltpu.VMEM((8, 2, n), f32), pltpu.VMEM((n, LANES), f32), pltpu.VMEM((n, LANES), f32), pltpu.VMEM((n, d), f32),
                pltpu.VMEM((n, LANES), f32), pltpu.VMEM((2, TILE, chunk), bf16)]
            if final:
                scratch += [pltpu.VMEM((2, n, d), f32), pltpu.VMEM((2, n, LANES), f32)]
            scratch += [dma((4,)), dma((count,))] + ([dma((4,)), dma((n // LANES,))] if final else [dma((2,))])
            old = old or ()
            return pl.pallas_call(
                functools.partial(pair_kernel, parts, final, by_task),
                out_shape=(sums[0], jax.ShapeDtypeStruct((8, LANES), f32)) if final else sums,
                in_specs=[smem] + [hbm] * (4 + len(sources) + len(old)),
                out_specs=(hbm, vmem) if final else (hbm, hbm),
                scratch_shapes=scratch,
                compiler_params=pltpu.CompilerParams(vmem_limit_bytes=60 * 2**20),
                cost_estimate=cost(count),
                name='far_pairs' if final else 'ring_pairs',
            )(pair_band, positions, a_col, q_col, *sources, meta, *old)

        rest = CHUNKS - 1
        ring_parts = (
            (None, 1, rest, 1, lambda core: reach - 2), (None, 1, rest, 2, lambda core: reach + 2),
            (None, 1, rest, 3, lambda core: reach - 1 - 2 * core), (None, 1, rest, 4, lambda core: reach + 3 - 2 * core))
        acc_b, row_b = pairs(ring_parts, (left, right, left_x, right_x), None)
        far_parts = ((0, 0, CHUNKS, 5, lambda core: 2 * reach * core), (1, 0, CHUNKS, 5, lambda core: 2 * reach * core))
        forces, share = pairs(far_parts, (far_up, far_down), (acc_a, row_a, acc_b, row_b))
        energy = pl.pallas_call(
            functools.partial(energy_kernel, seg_len),
            out_shape=jax.ShapeDtypeStruct((8, LANES), f32),
            in_specs=[vmem],
            out_specs=vmem,
            scratch_shapes=[pltpu.VMEM((seg_len, 8, LANES), f32), dma((seg_len,)), dma((seg_len,))],
            compiler_params=pltpu.CompilerParams(collective_id=1, has_side_effects=True),
            name='energy',
        )(share)
        return forces, energy[0, 0].reshape(1)

    row_spec = P(('sys', 'seg'), None)
    vec_spec = P(('sys', 'seg'))
    return jax.shard_map(device_fn, mesh=mesh, in_specs=(row_spec, vec_spec, row_spec), out_specs=(row_spec, P('sys')), check_vma=False)
```

time: 202 us -> 252 us (1.25)
  Pallas kernels: 193 us -> 243 us
  local copies, waits for them, and re-layouts: 7.38 us -> 2.84 us
  starting transfers between devices: 0 us -> 4.33 us
    pallas_call x1 -> x4, Pallas kernels: 193 us -> 243 us  [the longest x2 149 us: pairs(): pl.pallas_call(functools.partial(pair_kernel, parts, final, by_task), out...]
    unnamed x1 -> x2, local copies, waits for them, and re-layouts: 6.2 us -> 1.64 us
    ppermute x0 -> x2, starting transfers between devices: none -> 4.33 us  [the longest x1 2.84 us: device_fn(): far_up = lax.ppermute(left, 'seg', ups)]
  transfers between devices with their start and end apart: 0 -> 2, of which waited for: 0 -> 0; matrix products, arithmetic and copies ran while one was open for 0% -> 0% of each run, Pallas kernels for 0% -> 43%
where the time goes in v3:
time: 252 us; the launch traced here: 251 us
  Pallas kernels  243 us (96%)
  starting transfers between devices  4.33 us (2%)
  local copies, waits for them, and re-layouts  2.84 us (1%)
    pallas_call x2, Pallas kernels, pairs(): pl.pallas_call(functools.partial(pair_kernel, parts, final, by_task), out...  149 us
    pallas_call x1, Pallas kernels, device_fn(): pl.pallas_call(functools.partial(gather_kernel, seg_len, reach), out_shap...  82.9 us
    pallas_call x1, Pallas kernels, device_fn(): pl.pallas_call(functools.partial(energy_kernel, seg_len), out_shape=jax.S...  11.1 us
  transfers between devices with their start and end apart: 2, of which 0 were waited for; matrix products, arithmetic and copies ran while one was open for 0% of the time, Pallas kernels for 43%

profile of v3, /device:TPU:81, one launch (start us, length us, event | category | flops | bytes accessed | tf_op | source)
XLA Modules:
  0.0 251.3 jit_solution(12314355976155506093)
XLA Ops:
  0.6 82.9 %gather_pairs.1 = (f32[3072,512]{1,0:T(8,128)}, f32[3072,128]{1,0:T(8,128)}, f32[3072,128]{1,0:T(8,128)}, f32[3072,128]{1,0:T(8,128)}, f32[8,2,3072]{2,1,0:T(2,1...) custom-call(s32[1,7]{1,0:T(1,128)} %band_ref.5, ...), custom_call_target="tpu_custom_call" | custom-call | flops 51539607552 | bytes 25165824 | tf_op jit(solution)/shard_map/gather_pairs/pallas_call | solution.py:526
  83.5 2.8 %collective-permute-start = (bf16[3072,512]{1,0:T(8,128)(2,1)}, bf16[3072,512]{1,0:T(8,128)(2,1)S(1)}, u32[]{:S(2)}, u32[]{:S(2)}) collective-permute-start(bf16[3072,512]{1,0:T(8,128)(2,1)} %get-tuple-element.17.refs_0_), channel_id=1, source_target_pairs={{1,2},{3,4},{5,6},{7,0},{9,10},{11,12},{13,14},{15,8},{17,18},{19,... | collective-permute-start | bytes 9437192 | tf_op jit(solution)/shard_map/ppermute | solution.py:551
  86.4 1.5 collective-permute-start.1
  87.9 107.1 %ring_pairs.1 = (f32[3072,512]{1,0:T(8,128)}, f32[3072,128]{1,0:T(8,128)}) custom-call(s32[1,7]{1,0:T(1,128)} %band_ref.5, bf16[3072,512]{1,0:T(8,128)(2,1)} %x_hbm.5, f32[3072,128]{1,0:T(8,128)} %get-tuple-element.15.a_hbm, f32[3072,128]{1,0:T(8,128)} %get-tuple-element.16.q_hbm, bf16[3072,512]{1,0:T(8,128)(2,1)} %get-tuple-element.17.refs_0_, ...), custom_call_target="tpu_custom_call" | custom-call | flops 64424509440 | bytes 25165824 | tf_op jit(solution)/shard_map/ring_pairs/pallas_call | solution.py:565
  194.9 0.0 collective-permute-done.refs_0_
  195.0 0.0 copy-start
  195.0 0.0 collective-permute-done.1.refs_1_
  195.0 1.6 copy-done
  196.6 42.3 %far_pairs.1 = (f32[3072,512]{1,0:T(8,128)}, f32[8,128]{1,0:T(8,128)}) custom-call(s32[1,7]{1,0:T(1,128)} %band_ref.5, bf16[3072,512]{1,0:T(8,128)(2,1)} %x_hbm.5, f32[3072,128]{1,0:T(8,128)} %get-tuple-element.15.a_hbm, f32[3072,128]{1,0:T(8,128)} %get-tuple-element.16.q_hbm, bf16[3072,512]{1,0:T(8,128)(2,1)} %copy-done, ...), custom_call_target="tpu_custom_call" | custom-call | flops 19327352832 | bytes 25165824 | tf_op jit(solution)/shard_map/far_pairs/pallas_call | solution.py:565
  238.9 11.1 %energy.1 = f32[8,128]{1,0:T(8,128)} custom-call(f32[8,128]{1,0:T(8,128)} %get-tuple-element.27.e_in), custom_call_target="tpu_custom_call" | custom-call | tf_op jit(solution)/shard_map/energy/pallas_call | solution.py:583
  250.1 1.2 slice.3
Async XLA Ops:
  83.5 111.4 %collective-permute-start = (bf16[3072,512]{1,0:T(8,128)(2,1)}, bf16[3072,512]{1,0:T(8,128)(2,1)S(1)}, u32[]{:S(2)}, u32[]{:S(2)}) collective-permute-start(bf16[3072,512]{1,0:T(8,128)(2,1)} %get-tuple-element.17.refs_0_), channel_id=1, source_target_pairs={{1,2},{3,4},{5,6},{7,0},{9,10},{11,12},{13,14},{15,8},{17,18},{19,... | collective-permute-start | bytes 9437192 | tf_op jit(solution)/shard_map/ppermute | solution.py:551
  86.4 108.6 %collective-permute-start.1 = (bf16[3072,512]{1,0:T(8,128)(2,1)}, bf16[3072,512]{1,0:T(8,128)(2,1)}, u32[]{:S(2)}, u32[]{:S(2)}) collective-permute-start(bf16[3072,512]{1,0:T(8,128)(2,1)} %get-tuple-element.18.refs_1_), channel_id=1, source_target_pairs={{0,7},{2,1},{4,3},{6,5},{8,15},{10,9},{12,11},{14,13},{16,23},{18,... | collective-permute-start | bytes 9437192 | tf_op jit(solution)/shard_map/ppermute | solution.py:552
  195.0 1.7 copy-start
